TPU v7x, 256 devices: a whole 4x4x8 slice. The times are simulated.
256 devices in a mesh: prow: 8 (over y, core), pcol: 32 (over x, z).
Axes of the slice: x: 4, y: 4, z: 8, core: 2. Of those that a mesh axis runs over, the one named last changes fastest.
Arguments:
- matrix: bfloat16 [2, 8, 8, 256, 2, 32, 256], P(None, None, 'prow', None, None, 'pcol'), may hold values from -6 to 6
Outputs:
- image: float32 [2, 8, 8, 256, 2, 32, 256], P(None, None, 'prow', None, None, 'pcol')
All inputs are finite; a program needn't handle non-finite values.
Results may differ from a plain program's by a relative error of at most 0.0003.
Values sent between devices are 32-bit elements; how exact they have to be, the bound alone decides.
A program may use at most 64 MiB of HBM per device.

v0:
```python
import jax
import jax.numpy as jnp
from jax import lax
from jax.sharding import PartitionSpec as P

HIGH = lax.Precision.HIGHEST


def sent_to_all(value, axis):
    copies = jnp.broadcast_to(value, (lax.axis_size(axis), *value.shape))
    return lax.all_to_all(copies, axis, split_axis=0, concat_axis=0, tiled=True)


def in_order(pieces, dim):
    dims = list(pieces.shape[1:])
    dims[dim] *= pieces.shape[0]
    return jnp.moveaxis(pieces, 0, dim).reshape(dims)


def collect(value, axis, dim):
    pieces = sent_to_all(value, axis)
    return in_order(pieces, dim)


def shards(matrix):
    batch = matrix.shape[0]
    rows_here = matrix.shape[1]
    tile_len = matrix.shape[3]
    cols_here = matrix.shape[4]
    prow_count = lax.axis_size("prow")
    pcol_count = lax.axis_size("pcol")
    prow_index = lax.axis_index("prow")
    pcol_index = lax.axis_index("pcol")
    local = matrix.astype(jnp.float32).reshape(batch, rows_here, tile_len, cols_here, tile_len)
    first_idx = lax.broadcasted_iota(jnp.int32, (tile_len, tile_len), 0)
    second_idx = lax.broadcasted_iota(jnp.int32, (tile_len, tile_len), 1)
    upper = (first_idx <= second_idx).astype(jnp.float32)
    lower = (second_idx <= first_idx).astype(jnp.float32)
    rowscan = jnp.einsum("nrick,kj->nricj", local, upper, precision=HIGH)
    row_sums = rowscan[:, :, :, :, tile_len - 1]
    gathered = collect(row_sums, "pcol", 3)
    source = jnp.arange(pcol_count * cols_here, dtype=jnp.int32)
    source_glob = source % cols_here * pcol_count + source // cols_here
    target_glob = jnp.arange(cols_here, dtype=jnp.int32) * pcol_count + pcol_index
    earlier_mask = (source_glob[:, None] < target_glob[None, :]).astype(jnp.float32)
    row_carry = jnp.einsum("nrig,gc->nric", gathered, earlier_mask, precision=HIGH)
    rowscan = rowscan + row_carry[:, :, :, :, None]
    colscan = jnp.einsum("ik,nrkcj->nricj", lower, rowscan, precision=HIGH)
    col_sums = colscan[:, :, tile_len - 1, :, :]
    gathered = collect(col_sums, "prow", 1)
    source = jnp.arange(prow_count * rows_here, dtype=jnp.int32)
    source_glob = source % rows_here * prow_count + source // rows_here
    target_glob = jnp.arange(rows_here, dtype=jnp.int32) * prow_count + prow_index
    earlier_mask = (source_glob[:, None] < target_glob[None, :]).astype(jnp.float32)
    col_carry = jnp.einsum("ngcj,gr->nrcj", gathered, earlier_mask, precision=HIGH)
    colscan = colscan + col_carry[:, :, None, :, :]
    row_glob = (
        jnp.arange(rows_here, dtype=jnp.int32)[:, None] * prow_count + prow_index
    ) * tile_len + jnp.arange(tile_len, dtype=jnp.int32)[None, :]
    col_glob = (
        jnp.arange(cols_here, dtype=jnp.int32)[:, None] * pcol_count + pcol_index
    ) * tile_len + jnp.arange(tile_len, dtype=jnp.int32)[None, :]
    row_factor = 1.0 / jnp.sqrt(row_glob.astype(jnp.float32) + 1.0)
    col_factor = 1.0 / jnp.sqrt(col_glob.astype(jnp.float32) + 1.0)
    scaled = colscan * (row_factor[None, :, :, None, None] * col_factor[None, None, None, :, :])
    return scaled.reshape(batch, rows_here, 1, tile_len, cols_here, 1, tile_len)


def solution(mesh):
    return jax.shard_map(
        shards,
        mesh=mesh,
        in_specs=(P(None, None, "prow", None, None, "pcol", None),),
        out_specs=P(None, None, "prow", None, None, "pcol", None),
        check_vma=False,
    )
```

profile of v0, /device:TPU:1, one launch (start us, length us, event | category | flops | bytes accessed | tf_op | source)
XLA Modules:
  0.0 88.6 jit_solution(3840705140962412589)
XLA Ops:
  0.0 3.5 %fusion.8 = f32[2,8,256,2,256]{2,4,3,1,0:T(8,128)S(1)} fusion(bf16[2,8,256,2,256]{4,3,2,1,0:T(2,128)(2,1)} %bitcast.45), kind=kOutput, calls=%fused_computation.7 | convolution fusion | flops 1073807360 | bytes 12582912 | tf_op jit(solution)/shard_map/nrick,kj->nricj/dot_general | solution.py:39
  3.5 0.0 copy-start.1
  3.5 3.4 %copy-done.1 = f32[2,8,256,2,256]{2,4,3,1,0:T(8,128)} copy-done((f32[2,8,256,2,256]{2,4,3,1,0:T(8,128)}, f32[2,8,256,2,256]{2,4,3,1,0:T(8,128)S(1)}, u32[]{:S(2)}) %copy-start.1) | copy-done | bytes 8388632
  6.9 1.1 %broadcast_in_dim.4 = f32[32,2,8,256,2]{3,2,4,1,0:T(8,128)} broadcast(f32[2,8,256,2]{2,1,3,0:T(8,128)S(1)} %bitcast.47), dimensions={1,2,3,4} | broadcast | bytes 1081344 | tf_op jit(solution)/shard_map/broadcast_in_dim | solution.py:10
  8.0 11.9 %all-to-all-start = ((f32[32,2,8,256,2]{3,2,4,1,0:T(8,128)}), f32[32,2,8,256,2]{3,2,4,1,0:T(8,128)S(1)}, u32[]{:S(2)}, u32[]{:S(2)}) async-start(f32[32,2,8,256,2]{3,2,4,1,0:T(8,128)} %broadcast_in_dim.4), calls=%async_computation | async-start | bytes 2097152 | tf_op jit(solution)/shard_map/all_to_all | solution.py:11
  20.0 0.1 add_rsqrt_fusion.1
  20.1 0.1 add_rsqrt_fusion
  20.1 24.6 %all-to-all-done = f32[32,2,8,256,2]{3,2,4,1,0:T(8,128)S(1)} async-done(((f32[32,2,8,256,2]{3,2,4,1,0:T(8,128)}), f32[32,2,8,256,2]{3,2,4,1,0:T(8,128)S(1)}, u32[]{:S(2)}, u32[]{:S(2)}) %all-to-all-start) | async-done | bytes 1048608 | tf_op jit(solution)/shard_map/all_to_all | solution.py:11
  44.7 0.1 copy.16
  44.8 0.7 fusion.11
  45.6 7.3 %fusion.5 = f32[2,8,256,2,256]{4,2,3,1,0:T(8,128)S(1)} fusion(f32[2,8,256,2,256]{2,4,3,1,0:T(8,128)} %copy-done.1, f32[2,8,256,2]{2,3,1,0:T(2,128)S(1)} %fusion.11), kind=kOutput, calls=%fused_computation.6 | convolution fusion | flops 6444613632 | bytes 16809984 | tf_op jit(solution)/shard_map/ik,nrkcj->nricj/dot_general | solution.py:48
  52.8 0.0 copy-start
  52.8 3.4 %copy-done = f32[2,8,256,2,256]{4,2,3,1,0:T(8,128)} copy-done((f32[2,8,256,2,256]{4,2,3,1,0:T(8,128)}, f32[2,8,256,2,256]{4,2,3,1,0:T(8,128)S(1)}, u32[]{:S(2)}) %copy-start) | copy-done | bytes 8388632
  56.3 0.7 broadcast_in_dim.5
  57.0 9.2 %all-to-all-start.1 = ((f32[8,2,8,2,256]{4,2,3,1,0:T(8,128)}), f32[8,2,8,2,256]{4,2,3,1,0:T(8,128)S(1)}, u32[]{:S(2)}, u32[]{:S(2)}) async-start(f32[8,2,8,2,256]{4,2,3,1,0:T(8,128)} %broadcast_in_dim.5), calls=%async_computation.1 | async-start | bytes 524288 | tf_op jit(solution)/shard_map/all_to_all | solution.py:11
  66.2 2.3 %broadcast_multiply_fusion = f32[8,256,2,256]{3,1,2,0:T(8,128)} fusion(f32[2,256]{1,0:T(2,128)S(1)} %add_rsqrt_fusion.1, f32[8,256]{1,0:T(8,128)S(1)} %add_rsqrt_fusion), kind=kLoop, calls=%fused_computation.8 | loop fusion | flops 1048576 | bytes 4204544 | tf_op jit(solution)/shard_map/mul | solution.py:65
  68.5 4.2 %all-to-all-done.1 = f32[8,2,8,2,256]{4,2,3,1,0:T(8,128)S(1)} async-done(((f32[8,2,8,2,256]{4,2,3,1,0:T(8,128)}), f32[8,2,8,2,256]{4,2,3,1,0:T(8,128)S(1)}, u32[]{:S(2)}, u32[]{:S(2)}) %all-to-all-start.1) | async-done | bytes 262176 | tf_op jit(solution)/shard_map/all_to_all | solution.py:11
  72.7 0.2 convolution_bitcast_fusion
  72.9 5.8 %multiply_bitcast_fusion = f32[2,8,1,256,2,1,256]{6,3,4,1,0,5,2:T(8,128)S(1)} fusion(f32[2,8,256,2,256]{4,2,3,1,0:T(8,128)} %copy-done, f32[8,256,2,256]{3,1,2,0:T(8,128)} %broadcast_multiply_fusion, f32[2,8,2,256]{3,2,1,0:T(2,128)S(1)} %copy.21), kind=kLoop, calls=%fused_computation | loop fusion | flops 4194304 | bytes 21004288 | tf_op jit(solution)/shard_map/reshape | solution.py:66
  78.7 9.9 %copy.22 = f32[2,8,1,256,2,1,256]{6,5,4,3,2,1,0:T(1,128)} copy(f32[2,8,1,256,2,1,256]{6,3,4,1,0,5,2:T(8,128)S(1)} %multiply_bitcast_fusion) | data formatting | bytes 16777216 | tf_op jit(solution)/shard_map/reshape | solution.py:66
  (11 shorter events, 0.1 us)
Async XLA Ops:
  3.5 3.4 %copy-start.1 = (f32[2,8,256,2,256]{2,4,3,1,0:T(8,128)}, f32[2,8,256,2,256]{2,4,3,1,0:T(8,128)S(1)}, u32[]{:S(2)}) copy-start(f32[2,8,256,2,256]{2,4,3,1,0:T(8,128)S(1)} %fusion.8) | copy-start | bytes 25165828
  8.0 36.7 %all-to-all-start = ((f32[32,2,8,256,2]{3,2,4,1,0:T(8,128)}), f32[32,2,8,256,2]{3,2,4,1,0:T(8,128)S(1)}, u32[]{:S(2)}, u32[]{:S(2)}) async-start(f32[32,2,8,256,2]{3,2,4,1,0:T(8,128)} %broadcast_in_dim.4), calls=%async_computation | async-start | bytes 2097152 | tf_op jit(solution)/shard_map/all_to_all | solution.py:11
  52.8 3.4 %copy-start = (f32[2,8,256,2,256]{4,2,3,1,0:T(8,128)}, f32[2,8,256,2,256]{4,2,3,1,0:T(8,128)S(1)}, u32[]{:S(2)}) copy-start(f32[2,8,256,2,256]{4,2,3,1,0:T(8,128)S(1)} %fusion.5) | copy-start | bytes 25165828
  57.0 15.7 %all-to-all-start.1 = ((f32[8,2,8,2,256]{4,2,3,1,0:T(8,128)}), f32[8,2,8,2,256]{4,2,3,1,0:T(8,128)S(1)}, u32[]{:S(2)}, u32[]{:S(2)}) async-start(f32[8,2,8,2,256]{4,2,3,1,0:T(8,128)} %broadcast_in_dim.5), calls=%async_computation.1 | async-start | bytes 524288 | tf_op jit(solution)/shard_map/all_to_all | solution.py:11
where the time goes:
time: 89 us; the launch traced here: 88.6 us
  waiting for transfers between devices  28.8 us (32%)
  starting transfers between devices  21 us (24%)
  local copies, waits for them, and re-layouts  18.7 us (21%)
  matrix products  11.7 us (13%)
  other arithmetic  8.28 us (9%)
    all_to_all x2, waiting for transfers between devices, sent_to_all(): return lax.all_to_all(copies, axis, split_axis=0, concat_axis=0, tiled=True)  28.8 us
    all_to_all x2, starting transfers between devices, sent_to_all(): return lax.all_to_all(copies, axis, split_axis=0, concat_axis=0, tiled=True)  21 us
    reshape x1, local copies, waits for them, and re-layouts, shards(): return scaled.reshape(batch, rows_here, 1, tile_len, cols_here, 1, tile_len)  9.91 us
    dot_general x1, matrix products, shards(): colscan = jnp.einsum('ik,nrkcj->nricj', lower, rowscan, precision=HIGH)  7.27 us
    unnamed x4, local copies, waits for them, and re-layouts  6.78 us
    reshape x1, other arithmetic, shards(): return scaled.reshape(batch, rows_here, 1, tile_len, cols_here, 1, tile_len)  5.82 us
    dot_general x1, matrix products, shards(): rowscan = jnp.einsum('nrick,kj->nricj', local, upper, precision=HIGH)  3.48 us
    mul x1, other arithmetic, shards(): row_factor[None, :, :, None, None] * col_factor[None, None, None, :, :]  2.27 us
  transfers between devices with their start and end apart: 2, of which 2 were waited for; matrix products, arithmetic and copies ran while one was open for 3% of the time, Pallas kernels for 0%

commit v1 on v0

v1 whole, which is shorter than its diff:
```python
import jax
import jax.numpy as jnp
from jax import lax
from jax.experimental import pallas as pl
from jax.experimental.pallas import tpu as pltpu
from jax.sharding import PartitionSpec as P

MESH = pl.DeviceIdType.MESH
F32, BF16 = jnp.float32, jnp.bfloat16
NI, NR, NC, B = 2, 8, 2, 256
NP, NX, NZ = 8, 4, 8
CHUNK = 4 * B
ROWS = NI * NR * CHUNK
BLOCKS = NI * NR * NC


def iota(shape, dim):
    return lax.broadcasted_iota(jnp.int32, shape, dim)


def dot(a, b, dims):
    return lax.dot_general(a, b, (dims, ((), ())), preferred_element_type=F32)


def split3(v):
    hi = v.astype(BF16)
    rest = v - hi.astype(F32)
    mid = rest.astype(BF16)
    low = (rest - mid.astype(F32)).astype(BF16)
    return hi, mid, low


def scan_kernel(
    x_hbm, l_ref, carry_ref, bt_ref,
    xv, fbuf, xb, rs, cs, tot, z1, x2, ca, ps, ts, tp, cp, vs, vz, vt, vx, cb,
    in_sem, z1_s, z1_r, x2_s, x2_r, ca_s, ca_r, tp_s, tp_r, cp_s, cp_r, vz_s, vz_r, vx_s, vx_r,
):
    p = lax.axis_index("prow")
    q = lax.axis_index("pcol")
    x, z = q // NZ, lax.rem(q, NZ)

    def z_mate(d):
        zz = lax.rem(z + d, NZ)
        return zz, (p, x * NZ + zz)

    def x_mate(d):
        xx = lax.rem(x + d, NX)
        return xx, (p, xx * NZ + z)

    def p_mate(d):
        pp = lax.rem(p + d, NP)
        return pp, (pp, q)

    z_order = (4, 3, 5, 2, 6, 1, 7)
    x_order = (2, 1, 3)
    p_order = (4, 5, 3, 2, 6, 7, 1)

    loads = []
    for r in range(NR):
        for n in range(NI):
            k = n * NR + r
            rows = pl.ds(k * CHUNK, CHUNK)
            copy = pltpu.make_async_copy(x_hbm.at[rows], xv.at[rows], in_sem.at[k])
            copy.start()
            loads.append(copy)

    barrier = pltpu.get_barrier_semaphore()
    for mate, order in ((z_mate, z_order), (x_mate, x_order), (p_mate, p_order)):
        for d in order:
            pl.semaphore_signal(barrier, inc=1, device_id=mate(d)[1], device_id_type=MESH)

    def copies(mate, order, src_of, dst, send, recv, me):
        out = []
        for d in order:
            other, device = mate(d)
            out.append(pltpu.make_async_remote_copy(
                src_ref=src_of(other), dst_ref=dst.at[me], send_sem=send.at[d], recv_sem=recv.at[me],
                device_id=device, device_id_type=MESH))
        return out

    def start(group):
        for c in group:
            c.start()

    def wait_recv(mate, order, src_of, dst, send, recv):
        for d in order:
            other, device = mate(d)
            pltpu.make_async_remote_copy(
                src_ref=src_of(other), dst_ref=dst.at[other], send_sem=send.at[d], recv_sem=recv.at[other],
                device_id=device, device_id_type=MESH).wait_recv()

    def wait_send(group):
        for c in group:
            c.wait_send()

    sub = iota((8, 128), 0)
    lane = iota((8, 128), 1)
    zero = jnp.zeros((8, 128), F32)
    row16 = iota((16, B), 0)
    one_hot = [jnp.where((row16 == k) | (row16 == k + 4), 1.0, 0.0).astype(BF16) for k in range(4)]

    totals = zero
    for r in range(NR):
        acc = jnp.zeros((16, B), F32)
        sums = []
        for n in range(NI):
            k = n * NR + r
            loads[r * NI + n].wait()
            f = xv[pl.ds(k * CHUNK, CHUNK), :].astype(F32)
            fbuf[n] = f
            s = jnp.sum(f.reshape(CHUNK // 64, 64, 128), axis=0)
            s = jnp.sum(s.reshape(8, 8, 128), axis=0)
            sums.append(s + pltpu.roll(s, 4, 0))
            for c in range(NC):
                left = fbuf[n, pl.ds(c, B, stride=4), :]
                right = fbuf[n, pl.ds(2 + c, B, stride=4), :]
                block = jnp.concatenate([left, right], axis=1).astype(BF16)
                xb[k * NC + c] = block
                acc += dot(one_hot[n * NC + c], block, ((1,), (1,)))
        rs[r] = jnp.where(sub < 4, acc[:8, :128], acc[:8, 128:])
        col = jnp.where(sub < 4, sums[0], sums[1])
        cs[r] = col
        totals = totals + jnp.where(lane == r, jnp.sum(col, axis=1, keepdims=True), 0.0)
    bt_bit = (sub // 2) % 2
    totals = totals + jnp.where(bt_bit == 0, pltpu.roll(totals, 6, 0), pltpu.roll(totals, 2, 0))
    tot[...] = totals
    z1[z] = rs[z]
    tp[p] = totals
    cp[p] = cs[...]

    pl.semaphore_wait(barrier, len(z_order) + len(x_order) + len(p_order))
    z1_src, tp_src, cp_src = (lambda o: rs.at[o]), (lambda o: tot), (lambda o: cs)
    z1_c = copies(z_mate, z_order, z1_src, z1, z1_s, z1_r, z)
    start(z1_c)
    tp_c = copies(p_mate, p_order, tp_src, tp, tp_s, tp_r, p)
    start(tp_c)
    cp_c = copies(p_mate, p_order, cp_src, cp, cp_s, cp_r, p)
    start(cp_c)

    upper = jnp.where(iota((B, B), 0) <= iota((B, B), 1), 1.0, 0.0).astype(BF16)
    lower = jnp.where(iota((B, B), 1) <= iota((B, B), 0), 1.0, 0.0).astype(BF16)

    def local_prefix(first, last):
        def body(i, _):
            u = dot(xb[i], upper, ((1,), (0,)))
            hi = u.astype(BF16)
            low = (u - hi.astype(F32)).astype(BF16)
            l_ref[pl.ds(i * B, B), :] = dot(lower, hi, ((1,), (0,))) + dot(lower, low, ((1,), (0,)))
            return 0
        lax.fori_loop(first, last, body, 0)

    local_prefix(0, 6)

    wait_recv(p_mate, p_order, tp_src, tp, tp_s, tp_r)
    every, before = zero, zero
    for i in range(NP):
        t = tp[i]
        every = every + t
        before = before + jnp.where(i < p, t, 0.0)
    for step in (1, 2, 4):
        every = every + jnp.where(lane >= step, pltpu.roll(every, step, 1), 0.0)
    v = before + jnp.where(lane >= 1, pltpu.roll(every, 1, 1), 0.0)
    vs[...] = v
    vz[z] = v
    vz_src = lambda o: vs
    vz_c = copies(z_mate, z_order, vz_src, vz, vz_s, vz_r, z)
    start(vz_c)

    local_prefix(6, 10)

    wait_recv(z_mate, z_order, z1_src, z1, z1_s, z1_r)
    run = zero
    prefix = []
    for i in range(NZ):
        prefix.append(run)
        run = run + z1[i]
    ts[...] = run
    x2[x] = run
    x2_src = lambda o: ts
    x2_c = copies(x_mate, x_order, x2_src, x2, x2_s, x2_r, x)
    start(x2_c)
    for i in range(NZ):
        ps[i] = prefix[i]

    local_prefix(10, 16)

    c_bit = sub % 2

    def x_base(ref):
        every, before = zero, zero
        for i in range(NX):
            t = ref[i]
            every = every + t
            before = before + jnp.where(i < x, t, 0.0)
        return before + jnp.where(c_bit == 1, pltpu.roll(every, 1, 0), 0.0)

    wait_recv(x_mate, x_order, x2_src, x2, x2_s, x2_r)
    base = x_base(x2)
    for i in range(NZ):
        ps[i] = ps[i] + base
    ca[z] = ps[z]
    ca_src = lambda o: ps.at[o]
    ca_c = copies(z_mate, z_order, ca_src, ca, ca_s, ca_r, z)
    start(ca_c)

    wait_recv(z_mate, z_order, vz_src, vz, vz_s, vz_r)
    every, before = zero, zero
    for i in range(NZ):
        t = vz[i]
        every = every + t
        before = before + jnp.where(i < z, t, 0.0)
    vt[...] = every
    vx[x] = every
    vx_src = lambda o: vt
    vx_c = copies(x_mate, x_order, vx_src, vx, vx_s, vx_r, x)
    start(vx_c)

    local_prefix(16, 22)

    wait_recv(p_mate, p_order, cp_src, cp, cp_s, cp_r)
    run = zero
    for r in range(NR):
        above = zero
        step = zero
        for i in range(NP):
            t = cp[i, r]
            step = step + t
            above = above + jnp.where(i < p, t, 0.0)
        cb[r] = run + above
        run = run + step
    half = jnp.where((iota((128, B), 0) <= iota((128, B), 1)), 1.0, 0.0).astype(BF16)
    scans = jnp.zeros((8 * NR, B), F32)
    for part in split3(cb[...].reshape(8 * NR, 128)):
        scans = scans + dot(part, half, ((1,), (0,)))
    cb[...] = scans[:, :128].reshape(NR, 8, 128)
    bt_ref[...] = scans[:, 128:].reshape(NR, 8, 128)
    for r in range(NR):
        cb[r] = cb[r] + jnp.where(bt_bit == 1, pltpu.roll(bt_ref[r], 2, 0), 0.0)

    local_prefix(22, BLOCKS)

    wait_recv(x_mate, x_order, vx_src, vx, vx_s, vx_r)
    corner = before + x_base(vx)
    for r in range(NR):
        bt_ref[r] = cb[r] + jnp.sum(jnp.where(lane == r, corner, 0.0), axis=1, keepdims=True)

    wait_recv(z_mate, z_order, ca_src, ca, ca_s, ca_r)
    carry_ref[...] = ca[...].reshape(8 * NR, 128)
    for group in (z1_c, tp_c, cp_c, vz_c, x2_c, ca_c, vx_c):
        wait_send(group)


def write_kernel(l_ref, carry_ref, bt_ref, o_hbm, at, stage, sem):
    p = lax.axis_index("prow")
    q = lax.axis_index("pcol")
    lower = jnp.where(iota((B, B), 1) <= iota((B, B), 0), 1.0, 0.0).astype(BF16)
    near = jnp.zeros((B, 8 * NR), F32)
    far = jnp.zeros((B, 8 * NR), F32)
    for part in split3(carry_ref[...]):
        near = near + dot(lower[:, :128], part, ((1,), (1,)))
        far = far + dot(lower[:, 128:], part, ((1,), (1,)))
    at[...] = near + pltpu.roll(far, 8 * NR - 4, 1)

    T = 64
    outs = []
    cf = [[lax.rsqrt(((c * NX * NZ + q) * B + bt * 128 + 1 + iota((1, 128), 1)).astype(F32)) for bt in range(2)] for c in range(NC)]
    for r in range(NR):
        for t in range(B // T):
            rf = lax.rsqrt(((r * NP + p) * B + t * T + 1 + iota((T, 128), 0)).astype(F32))
            for n in range(NI):
                k = n * NR + r
                for c in range(NC):
                    col = r * 8 + n * NC + c
                    av = jnp.broadcast_to(at[pl.ds(t * T, T), col:col + 1], (T, 128))
                    for bt in range(2):
                        bv = bt_ref[r, pl.ds(n * 4 + bt * 2 + c, 1), :]
                        lv = l_ref[pl.ds((k * NC + c) * B + t * T, T), pl.ds(bt * 128, 128)]
                        stage[pl.ds(k * CHUNK + t * T * 4 + c * 2 + bt, T, stride=4), :] = (lv + (av + bv)) * (rf * cf[c][bt])
        for n in range(NI):
            k = n * NR + r
            rows = pl.ds(k * CHUNK, CHUNK)
            copy = pltpu.make_async_copy(stage.at[rows], o_hbm.at[rows], sem.at[k])
            copy.start()
            outs.append(copy)
    for copy in outs:
        copy.wait()


def shards(matrix):
    rows = matrix.reshape(NI, NR, B, NC, 2, 128).transpose(0, 1, 2, 4, 3, 5).reshape(ROWS, 128)
    rows = pltpu.with_memory_space_constraint(rows, pltpu.HBM)
    hbm = pl.BlockSpec(memory_space=pltpu.HBM)
    vmem = pl.BlockSpec(memory_space=pltpu.VMEM)
    dma = pltpu.SemaphoreType.DMA
    tile = lambda *lead: pltpu.VMEM((*lead, 8, 128), F32)
    local, carry, bt = pl.pallas_call(
        scan_kernel,
        out_shape=(
            pltpu.VMEM((BLOCKS * B, B), F32),
            pltpu.VMEM((8 * NR, 128), F32),
            pltpu.VMEM((NR, 8, 128), F32),
        ),
        in_specs=[hbm],
        out_specs=(vmem, vmem, vmem),
        scratch_shapes=[
            pltpu.VMEM((ROWS, 128), BF16),
            pltpu.VMEM((NI, CHUNK, 128), F32),
            pltpu.VMEM((BLOCKS, B, B), BF16),
            tile(NR), tile(NR), tile(),
            tile(NZ), tile(NX), tile(NZ), tile(NZ), tile(),
            tile(NP), tile(NP, NR), tile(), tile(NZ), tile(), tile(NX), tile(NR),
            dma((NI * NR,)),
            dma((NZ,)), dma((NZ,)), dma((NX,)), dma((NX,)), dma((NZ,)), dma((NZ,)),
            dma((NP,)), dma((NP,)), dma((NP,)), dma((NP,)), dma((NZ,)), dma((NZ,)), dma((NX,)), dma((NX,)),
        ],
        compiler_params=pltpu.CompilerParams(collective_id=0, has_side_effects=True, vmem_limit_bytes=24 << 20),
        name="scan",
    )(rows)
    out = pl.pallas_call(
        write_kernel,
        out_shape=pltpu.HBM((ROWS, 128), F32),
        in_specs=[vmem, vmem, vmem],
        out_specs=hbm,
        scratch_shapes=[pltpu.VMEM((B, 8 * NR), F32), pltpu.VMEM((ROWS, 128), F32), dma((NI * NR,))],
        compiler_params=pltpu.CompilerParams(vmem_limit_bytes=24 << 20),
        name="write",
    )(local, carry, bt)
    return out.reshape(NI, NR, 1, B, NC, 1, B)


def solution(mesh):
    return jax.shard_map(
        shards,
        mesh=mesh,
        in_specs=(P(None, None, "prow", None, None, "pcol", None),),
        out_specs=P(None, None, "prow", None, None, "pcol", None),
        check_vma=False,
    )
```

time: 89 us -> 32.5 us (0.37)
  Pallas kernels: 0 us -> 32.4 us
  waiting for transfers between devices: 28.8 us -> 0 us
  starting transfers between devices: 21 us -> 0 us
  local copies, waits for them, and re-layouts: 18.7 us -> 0 us
  matrix products: 11.7 us -> 0 us
  other arithmetic: 8.28 us -> 0 us
    pallas_call x0 -> x2, Pallas kernels: none -> 32.4 us  [the longest x1 28 us: shards(): pl.pallas_call(scan_kernel, out_shape=(pltpu.VMEM((BLOCKS * B, B), F32),...]
    all_to_all x2 -> x0, waiting for transfers between devices: 28.8 us -> none  [sent_to_all(): return lax.all_to_all(copies, axis, split_axis=0, concat_axis=0, tiled=True)]
    all_to_all x2 -> x0, starting transfers between devices: 21 us -> none  [sent_to_all(): return lax.all_to_all(copies, axis, split_axis=0, concat_axis=0, tiled=True)]
    dot_general x4 -> x0, matrix products: 11.7 us -> none  [the longest x1 7.27 us: shards(): colscan = jnp.einsum('ik,nrkcj->nricj', lower, rowscan, precision=HIGH)]
    reshape x1 -> x0, local copies, waits for them, and re-layouts: 9.91 us -> none  [shards(): return scaled.reshape(batch, rows_here, 1, tile_len, cols_here, 1, tile_len)]
    unnamed x4 -> x0, local copies, waits for them, and re-layouts: 6.78 us -> none
    reshape x1 -> x0, other arithmetic: 5.82 us -> none  [shards(): return scaled.reshape(batch, rows_here, 1, tile_len, cols_here, 1, tile_len)]
    mul x3 -> x0, other arithmetic: 2.28 us -> none  [the longest x1 2.27 us: shards(): row_factor[None, :, :, None, None] * col_factor[None, None, None, :, :]]
  transfers between devices with their start and end apart: 2 -> 0, of which waited for: 2 -> 0; matrix products, arithmetic and copies ran while one was open for 3% -> 0% of each run, Pallas kernels for 0% -> 0%
where the time goes in v1:
time: 32.5 us; the launch traced here: 32.4 us
  Pallas kernels  32.4 us (100%)
    pallas_call x1, Pallas kernels, shards(): pl.pallas_call(scan_kernel, out_shape=(pltpu.VMEM((BLOCKS * B, B), F32),...  28 us
    pallas_call x1, Pallas kernels, shards(): pl.pallas_call(write_kernel, out_shape=pltpu.HBM((ROWS, 128), F32), in_sp...  4.4 us

profile of v1, /device:TPU:1, one launch (start us, length us, event | category | flops | bytes accessed | tf_op | source)
XLA Modules:
  0.0 32.4 jit_solution(2979907650069844174)
XLA Ops:
  0.0 28.0 %scan.1 = (f32[8192,256]{1,0:T(8,128)S(1)}, f32[64,128]{1,0:T(8,128)S(1)}, f32[8,8,128]{2,1,0:T(8,128)S(1)}) custom-call(bf16[16384,128]{1,0:T(8,128)(2,1)} %bitcast.6), custom_call_target="tpu_custom_call" | custom-call | tf_op jit(solution)/shard_map/scan/pallas_call | solution.py:296
  28.0 4.4 %write.1 = f32[16384,128]{1,0:T(8,128)} custom-call(f32[8192,256]{1,0:T(8,128)S(1)} %get-tuple-element.8.l_ref, f32[64,128]{1,0:T(8,128)S(1)} %get-tuple-element.9.carry_ref, f32[8,8,128]{2,1,0:T(8,128)S(1)} %get-tuple-element.10.bt_ref), custom_call_target="tpu_custom_call" | custom-call | tf_op jit(solution)/shard_map/write/pallas_call | solution.py:319

commit v2 on v1

v2 whole, which is shorter than its diff:
```python
import jax
import jax.numpy as jnp
from jax import lax
from jax.experimental import pallas as pl
from jax.experimental.pallas import tpu as pltpu
from jax.sharding import PartitionSpec as P

MESH = pl.DeviceIdType.MESH
F32, BF16 = jnp.float32, jnp.bfloat16
NI, NR, NC, B = 2, 8, 2, 256
NP, NX, NZ = 8, 4, 8
CHUNK = 4 * B
ROWS = NI * NR * CHUNK
BLOCKS = NI * NR * NC
SEG, PAD = CHUNK // 8, CHUNK // 8 + 8
STEPS = B // 8
GROUPS = 4


def iota(shape, dim):
    return lax.broadcasted_iota(jnp.int32, shape, dim)


def dot(a, b, dims):
    return lax.dot_general(a, b, (dims, ((), ())), preferred_element_type=F32)


def split3(v):
    hi = v.astype(BF16)
    rest = v - hi.astype(F32)
    mid = rest.astype(BF16)
    low = (rest - mid.astype(F32)).astype(BF16)
    return hi, mid, low


def rows_before(v):
    row = iota(v.shape, v.ndim - 2)
    for step in (1, 2, 4):
        v = v + jnp.where(row >= step, pltpu.roll(v, step, v.ndim - 2), 0.0)
    return jnp.where(row >= 1, pltpu.roll(v, 1, v.ndim - 2), 0.0)


def scan_kernel(
    x_hbm, l_ref, e_ref, carry_ref, bt_ref,
    xv, fbuf, rs, cs, tot, z1, x2, ca, ps, ts, tp, cp, vs, vz, vt, vx, cb,
    in_sem, send_sem, z1_r, x2_r, ca_r, tp_r, cp_r, vz_r, vx_r,
):
    p = lax.axis_index("prow")
    q = lax.axis_index("pcol")
    x, z = q // NZ, lax.rem(q, NZ)

    def z_mate(d):
        zz = lax.rem(z + d, NZ)
        return zz, (p, x * NZ + zz)

    def x_mate(d):
        xx = lax.rem(x + d, NX)
        return xx, (p, xx * NZ + z)

    def p_mate(d):
        pp = lax.rem(p + d, NP)
        return pp, (pp, q)

    z_order = (4, 3, 5, 2, 6, 1, 7)
    x_order = (2, 1, 3)
    p_order = (4, 5, 3, 2, 6, 7, 1)

    part = NR // GROUPS
    for g in range(GROUPS):
        for n in range(NI):
            rows = pl.ds((n * NR + g * part) * CHUNK, part * CHUNK)
            pltpu.make_async_copy(x_hbm.at[rows], xv.at[rows], in_sem.at[g]).start()

    barrier = pltpu.get_barrier_semaphore()
    for mate, order in ((z_mate, z_order), (x_mate, x_order), (p_mate, p_order)):
        for d in order:
            pl.semaphore_signal(barrier, inc=1, device_id=mate(d)[1], device_id_type=MESH)

    def send(mate, order, src_of, dst, recv, me):
        for d in order:
            other, device = mate(d)
            pltpu.make_async_remote_copy(
                src_ref=src_of(other), dst_ref=dst.at[me], send_sem=send_sem.at[0], recv_sem=recv.at[0],
                device_id=device, device_id_type=MESH).start()

    def receive(mate, order, dst, recv):
        every = dst.at[pl.ds(0, len(order))]
        pltpu.make_async_remote_copy(
            src_ref=every, dst_ref=every, send_sem=send_sem.at[0], recv_sem=recv.at[0],
            device_id=mate(1)[1], device_id_type=MESH).wait_recv()

    sub = iota((8, 128), 0)
    lane = iota((8, 128), 1)
    zero = jnp.zeros((8, 128), F32)
    row16, col16 = iota((16, B), 0), iota((16, B), 1)
    pick = [jnp.where((row16 // 8 == col16 // 128) & (row16 % 8 // 2 == t), 1.0, 0.0).astype(BF16) for t in range(4)]

    totals = zero
    for g in range(GROUPS):
      with jax.named_scope(f"sums{g}"):
        rows = pl.ds(g * NI * part * CHUNK, NI * part * CHUNK)
        pltpu.make_async_copy(x_hbm.at[rows], xv.at[rows], in_sem.at[g]).wait()
        for r in range(g * part, (g + 1) * part):
            acc = jnp.zeros((16, B), F32)
            for t in range(4):
                pair = [xv[pl.ds((n * NR + r) * CHUNK + t * B, B), :] for n in range(NI)]
                acc = acc + dot(pick[t], jnp.concatenate(pair, axis=1), ((1,), (1,)))
            sums = []
            for n in range(NI):
                f = xv[pl.ds((n * NR + r) * CHUNK, CHUNK), :].astype(F32)
                s = jnp.sum(f.reshape(CHUNK // 64, 64, 128), axis=0)
                s = jnp.sum(s.reshape(8, 8, 128), axis=0)
                sums.append(s + pltpu.roll(s, 4, 0))
            one, two = [jnp.where(sub % 2 == 0, acc[n * 8:n * 8 + 8, :128], acc[n * 8:n * 8 + 8, 128:]) for n in range(NI)]
            rs[r] = jnp.where(lane // 2 % 2 == 0, one + pltpu.roll(one, 126, 1), two + pltpu.roll(two, 2, 1))
            col = jnp.where(sub < 4, sums[0], sums[1])
            cs[r] = col
            totals = totals + jnp.where(lane == r, jnp.sum(col, axis=1, keepdims=True), 0.0)
    bt_bit = sub // 2 % 2
    totals = totals + jnp.where(bt_bit == 0, pltpu.roll(totals, 6, 0), pltpu.roll(totals, 2, 0))
    tot[...] = totals
    z1[z] = rs[z]
    tp[p] = totals
    cp[p] = cs[...]

    with jax.named_scope("barrier"):
        pl.semaphore_wait(barrier, len(z_order) + len(x_order) + len(p_order))
    send(z_mate, z_order, lambda o: rs.at[o], z1, z1_r, z)
    send(p_mate, p_order, lambda o: tot, tp, tp_r, p)
    send(p_mate, p_order, lambda o: cs, cp, cp_r, p)

    upper = jnp.where(iota((B, B), 0) <= iota((B, B), 1), 1.0, 0.0).astype(BF16)

    def local_prefix(first, last):
        def body(i, _):
            tiles = []
            for h in range(2):
                k = i * 2 + h
                for s in range(8):
                    fbuf[h, pl.ds(s * PAD, SEG), :] = xv[pl.ds(k * CHUNK + s * SEG, SEG), :].astype(F32)
                for c in range(NC):
                    halves = [jnp.concatenate([fbuf[h, pl.ds(j * 4 + bt * 2 + c, 8, stride=PAD), :] for j in range(STEPS)], axis=0) for bt in range(2)]
                    tiles.append((k * NC + c, jnp.concatenate(halves, axis=1).astype(BF16)))
            scans = [(b, dot(v, upper, ((1,), (0,)))) for b, v in tiles]
            for b, u in scans:
                run = jnp.zeros((8, B), F32)
                for j in range(STEPS):
                    run = run + u[j * 8:j * 8 + 8]
                    l_ref[pl.ds(b * B + j * 8, 8), :] = run
                e_ref[b] = rows_before(run)
            return 0
        with jax.named_scope(f"lp{first}"):
            lax.fori_loop(first, last, body, 0)

    local_prefix(0, 2)

    with jax.named_scope("wait_tp"):
        receive(p_mate, p_order, tp, tp_r)
    every, before = zero, zero
    for i in range(NP):
        t = tp[i]
        every = every + t
        before = before + jnp.where(i < p, t, 0.0)
    for step in (1, 2, 4):
        every = every + jnp.where(lane >= step, pltpu.roll(every, step, 1), 0.0)
    v = before + jnp.where(lane >= 1, pltpu.roll(every, 1, 1), 0.0)
    vs[...] = v
    vz[z] = v
    send(z_mate, z_order, lambda o: vs, vz, vz_r, z)

    local_prefix(2, 4)

    with jax.named_scope("wait_z1"):
        receive(z_mate, z_order, z1, z1_r)
    run = zero
    for i in range(NZ):
        ps[i] = run
        run = run + z1[i]
    ts[...] = run
    x2[x] = run
    send(x_mate, x_order, lambda o: ts, x2, x2_r, x)

    local_prefix(4, 6)

    def x_base(ref, axis, bit):
        every, before = zero, zero
        for i in range(NX):
            t = ref[i]
            every = every + t
            before = before + jnp.where(i < x, t, 0.0)
        return before + jnp.where(bit == 1, pltpu.roll(every, 1, axis), 0.0)

    with jax.named_scope("wait_x2"):
        receive(x_mate, x_order, x2, x2_r)
    base = x_base(x2, 1, lane % 2)
    for i in range(NZ):
        ps[i] = ps[i] + base
    ca[z] = ps[z]
    send(z_mate, z_order, lambda o: ps.at[o], ca, ca_r, z)

    with jax.named_scope("wait_vz"):
        receive(z_mate, z_order, vz, vz_r)
    every, before = zero, zero
    for i in range(NZ):
        t = vz[i]
        every = every + t
        before = before + jnp.where(i < z, t, 0.0)
    vt[...] = every
    vx[x] = every
    send(x_mate, x_order, lambda o: vt, vx, vx_r, x)

    local_prefix(6, 7)

    with jax.named_scope("wait_cp"):
        receive(p_mate, p_order, cp, cp_r)
    run = zero
    for r in range(NR):
        above, step = zero, zero
        for i in range(NP):
            t = cp[i, r]
            step = step + t
            above = above + jnp.where(i < p, t, 0.0)
        cb[r] = run + above
        run = run + step
    half = jnp.where(iota((128, B), 0) <= iota((128, B), 1), 1.0, 0.0).astype(BF16)
    scans = jnp.zeros((8 * NR, B), F32)
    for piece in split3(cb[...].reshape(8 * NR, 128)):
        scans = scans + dot(piece, half, ((1,), (0,)))
    cb[...] = scans[:, :128].reshape(NR, 8, 128)
    bt_ref[...] = scans[:, 128:].reshape(NR, 8, 128)
    for r in range(NR):
        cb[r] = cb[r] + jnp.where(bt_bit == 1, pltpu.roll(bt_ref[r], 2, 0), 0.0)

    local_prefix(7, 8)

    with jax.named_scope("wait_vx"):
        receive(x_mate, x_order, vx, vx_r)
    corner = before + x_base(vx, 0, sub % 2)
    for r in range(NR):
        bt_ref[r] = cb[r] + jnp.sum(jnp.where(lane == r, corner, 0.0), axis=1, keepdims=True)

    with jax.named_scope("wait_ca"):
        receive(z_mate, z_order, ca, ca_r)
    carry_ref[...] = ca[...].reshape(8 * NR, 128)
    tiles = 3 * len(z_order) + 2 * len(x_order) + (1 + NR) * len(p_order)
    sent = l_ref.at[pl.ds(0, tiles * 8 // 2)]
    with jax.named_scope("wait_send"):
        pltpu.make_async_remote_copy(
            src_ref=sent, dst_ref=sent, send_sem=send_sem.at[0], recv_sem=z1_r.at[0],
            device_id=z_mate(1)[1], device_id_type=MESH).wait_send()


def write_kernel(l_ref, e_ref, carry_ref, bt_ref, o_hbm, av, stage, sem):
    p = lax.axis_index("prow")
    q = lax.axis_index("pcol")
    src, dst = iota((128, B), 0), iota((128, B), 1)
    near = jnp.where((src % 4 == dst % 4) & ((src // 4 <= dst // 4) | (dst >= 128)), 1.0, 0.0).astype(BF16)
    scans = jnp.zeros((8 * NR, B), F32)
    for piece in split3(carry_ref[...]):
        scans = scans + dot(piece, near, ((1,), (0,)))
    av[...] = scans[:, :128].reshape(NR, 8, 128) + rows_before(scans[:, 128:].reshape(NR, 8, 128))

    cf = [[lax.rsqrt(((c * NX * NZ + q) * B + bt * 128 + 1 + iota((8, 128), 1)).astype(F32)) for bt in range(2)] for c in range(NC)]
    first_row = (p * B + 1 + iota((8, 128), 0) * STEPS).astype(F32)
    for r in range(NR):
        carry = av[r]
        offset = {}
        for n in range(NI):
            for c in range(NC):
                for bt in range(2):
                    own = e_ref[(n * NR + r) * NC + c][:, bt * 128:bt * 128 + 128]
                    offset[n, c, bt] = own + bt_ref[r, pl.ds(n * 4 + bt * 2 + c, 1), :]
        for j in range(STEPS):
            rf = lax.rsqrt(first_row + float(r * NP * B + j))
            scale = [[rf * cf[c][bt] for bt in range(2)] for c in range(NC)]
            for n in range(NI):
                k = n * NR + r
                for c in range(NC):
                    at = j * 4 + n * 2 + c
                    a = jnp.broadcast_to(carry[:, at:at + 1], (8, 128))
                    for bt in range(2):
                        lv = l_ref[pl.ds((k * NC + c) * B + j * 8, 8), pl.ds(bt * 128, 128)]
                        stage[pl.ds(k * 8 * PAD + j * 4 + c * 2 + bt, 8, stride=PAD), :] = (lv + (a + offset[n, c, bt])) * scale[c][bt]
        for n in range(NI):
            k = n * NR + r
            for s in range(8):
                pltpu.make_async_copy(
                    stage.at[pl.ds((k * 8 + s) * PAD, SEG)], o_hbm.at[pl.ds((k * 8 + s) * SEG, SEG)], sem.at[0]).start()
    pltpu.make_async_copy(stage.at[pl.ds(0, ROWS)], o_hbm, sem.at[0]).wait()


def shards(matrix):
    rows = matrix.reshape(NI, NR, B, NC, 2, 128).transpose(0, 1, 2, 4, 3, 5).reshape(ROWS, 128)
    rows = pltpu.with_memory_space_constraint(rows, pltpu.HBM)
    hbm = pl.BlockSpec(memory_space=pltpu.HBM)
    vmem = pl.BlockSpec(memory_space=pltpu.VMEM)
    dma = pltpu.SemaphoreType.DMA
    tile = lambda *lead: pltpu.VMEM((*lead, 8, 128), F32)
    found = pl.pallas_call(
        scan_kernel,
        out_shape=(
            pltpu.VMEM((BLOCKS * B, B), F32),
            pltpu.VMEM((BLOCKS, 8, B), F32),
            pltpu.VMEM((8 * NR, 128), F32),
            pltpu.VMEM((NR, 8, 128), F32),
        ),
        in_specs=[hbm],
        out_specs=(vmem, vmem, vmem, vmem),
        scratch_shapes=[
            pltpu.VMEM((ROWS, 128), BF16),
            pltpu.VMEM((2, 8 * PAD, 128), F32),
            tile(NR), tile(NR), tile(),
            tile(NZ), tile(NX), tile(NZ), tile(NZ), tile(),
            tile(NP), tile(NP, NR), tile(), tile(NZ), tile(), tile(NX), tile(NR),
            dma((GROUPS,)),
        ] + [dma((1,))] * 8,
        compiler_params=pltpu.CompilerParams(collective_id=0, has_side_effects=True, vmem_limit_bytes=24 << 20),
        name="scan",
    )(rows)
    out = pl.pallas_call(
        write_kernel,
        out_shape=pltpu.HBM((ROWS, 128), F32),
        in_specs=[vmem, vmem, vmem, vmem],
        out_specs=hbm,
        scratch_shapes=[tile(NR), pltpu.VMEM((NI * NR * 8 * PAD, 128), F32), dma((1,))],
        compiler_params=pltpu.CompilerParams(vmem_limit_bytes=24 << 20),
        name="write",
    )(*found)
    return out.reshape(NI, NR, 1, B, NC, 1, B)


def solution(mesh):
    return jax.shard_map(
        shards,
        mesh=mesh,
        in_specs=(P(None, None, "prow", None, None, "pcol", None),),
        out_specs=P(None, None, "prow", None, None, "pcol", None),
        check_vma=False,
    )
```

time: 32.5 us -> 26.1 us (0.80)
  Pallas kernels: 32.4 us -> 26.1 us
    pallas_call x1, Pallas kernels: 28 us -> 22 us  [shards(): pl.pallas_call(scan_kernel, out_shape=(pltpu.VMEM((BLOCKS * B, B), F32),...]
where the time goes in v2:
time: 26.1 us
  Pallas kernels  26.1 us (100%)
    pallas_call x1, Pallas kernels, shards(): pl.pallas_call(scan_kernel, out_shape=(pltpu.VMEM((BLOCKS * B, B), F32),...  22 us
    pallas_call x1, Pallas kernels, shards(): pl.pallas_call(write_kernel, out_shape=pltpu.HBM((ROWS, 128), F32), in_sp...  4.09 us

profile of v2, /device:TPU:1, one launch (start us, length us, event | category | flops | bytes accessed | tf_op | source)
XLA Modules:
  0.0 26.1 jit_solution(10775189964495617160)
XLA Ops:
  0.0 22.0 %scan.1 = (f32[8192,256]{1,0:T(8,128)S(1)}, f32[32,8,256]{2,1,0:T(8,128)S(1)}, f32[64,128]{1,0:T(8,128)S(1)}, f32[8,8,128]{2,1,0:T(8,128)S(1)}) custom-call(bf16[16384,128]{1,0:T(8,128)(2,1)} %bitcast.6), custom_call_target="tpu_custom_call" | custom-call | tf_op jit(solution)/shard_map/scan/pallas_call | solution.py:299
  22.0 4.1 %write.1 = f32[16384,128]{1,0:T(8,128)} custom-call(f32[8192,256]{1,0:T(8,128)S(1)} %get-tuple-element.9.l_ref, f32[32,8,256]{2,1,0:T(8,128)S(1)} %get-tuple-element.10.e_ref, f32[64,128]{1,0:T(8,128)S(1)} %get-tuple-element.11.carry_ref, f32[8,8,128]{2,1,0:T(8,128)S(1)} %get-tuple-element.12.bt_ref), custom_call_target="tpu_custom_call" | custom-call | tf_op jit(solution)/shard_map/write/pallas_call | solution.py:320

commit v3 on v2

--- a/solution.py
+++ b/solution.py
@@ -42,8 +42,8 @@
 
 def scan_kernel(
     x_hbm, l_ref, e_ref, carry_ref, bt_ref,
-    xv, fbuf, rs, cs, tot, z1, x2, ca, ps, ts, tp, cp, vs, vz, vt, vx, cb,
-    in_sem, send_sem, z1_r, x2_r, ca_r, tp_r, cp_r, vz_r, vx_r,
+    xv, fbuf, rs, cs, tot, z1, x2, ca, ps, ts, tp, cp, vs, vq, cb,
+    in_sem, send_sem, vq_s, z1_r, x2_r, ca_r, tp_r, cp_r, vq_r,
 ):
     p = lax.axis_index("prow")
     q = lax.axis_index("pcol")
@@ -61,9 +61,15 @@
         pp = lax.rem(p + d, NP)
         return pp, (pp, q)
 
+    def q_mate(d):
+        qq = lax.rem(x + d[0], NX) * NZ + lax.rem(z + d[1], NZ)
+        return qq, (p, qq)
+
     z_order = (4, 3, 5, 2, 6, 1, 7)
     x_order = (2, 1, 3)
     p_order = (4, 5, 3, 2, 6, 7, 1)
+    hops = lambda d: min(d[0], NX - d[0]) + min(d[1], NZ - d[1])
+    q_order = sorted([(a, b) for a in range(NX) for b in range(NZ) if a or b], key=hops, reverse=True)
 
     part = NR // GROUPS
     for g in range(GROUPS):
@@ -76,18 +82,18 @@
         for d in order:
             pl.semaphore_signal(barrier, inc=1, device_id=mate(d)[1], device_id_type=MESH)
 
-    def send(mate, order, src_of, dst, recv, me):
+    def send(mate, order, src_of, dst, recv, me, sent=send_sem):
         for d in order:
             other, device = mate(d)
             pltpu.make_async_remote_copy(
-                src_ref=src_of(other), dst_ref=dst.at[me], send_sem=send_sem.at[0], recv_sem=recv.at[0],
+                src_ref=src_of(other), dst_ref=dst.at[me], send_sem=sent.at[0], recv_sem=recv.at[0],
                 device_id=device, device_id_type=MESH).start()
 
     def receive(mate, order, dst, recv):
         every = dst.at[pl.ds(0, len(order))]
         pltpu.make_async_remote_copy(
             src_ref=every, dst_ref=every, send_sem=send_sem.at[0], recv_sem=recv.at[0],
-            device_id=mate(1)[1], device_id_type=MESH).wait_recv()
+            device_id=mate(order[0])[1], device_id_type=MESH).wait_recv()
 
     sub = iota((8, 128), 0)
     lane = iota((8, 128), 1)
@@ -115,9 +121,9 @@
             rs[r] = jnp.where(lane // 2 % 2 == 0, one + pltpu.roll(one, 126, 1), two + pltpu.roll(two, 2, 1))
             col = jnp.where(sub < 4, sums[0], sums[1])
             cs[r] = col
-            totals = totals + jnp.where(lane == r, jnp.sum(col, axis=1, keepdims=True), 0.0)
+            here = (lane == NR + r) | ((lane > r) & (lane < NR))
+            totals = totals + jnp.where(here, jnp.sum(col, axis=1, keepdims=True), 0.0)
     bt_bit = sub // 2 % 2
-    totals = totals + jnp.where(bt_bit == 0, pltpu.roll(totals, 6, 0), pltpu.roll(totals, 2, 0))
     tot[...] = totals
     z1[z] = rs[z]
     tp[p] = totals
@@ -152,23 +158,7 @@
         with jax.named_scope(f"lp{first}"):
             lax.fori_loop(first, last, body, 0)
 
-    local_prefix(0, 2)
-
-    with jax.named_scope("wait_tp"):
-        receive(p_mate, p_order, tp, tp_r)
-    every, before = zero, zero
-    for i in range(NP):
-        t = tp[i]
-        every = every + t
-        before = before + jnp.where(i < p, t, 0.0)
-    for step in (1, 2, 4):
-        every = every + jnp.where(lane >= step, pltpu.roll(every, step, 1), 0.0)
-    v = before + jnp.where(lane >= 1, pltpu.roll(every, 1, 1), 0.0)
-    vs[...] = v
-    vz[z] = v
-    send(z_mate, z_order, lambda o: vs, vz, vz_r, z)
-
-    local_prefix(2, 4)
+    local_prefix(0, 4)
 
     with jax.named_scope("wait_z1"):
         receive(z_mate, z_order, z1, z1_r)
@@ -180,36 +170,36 @@
     x2[x] = run
     send(x_mate, x_order, lambda o: ts, x2, x2_r, x)
 
-    local_prefix(4, 6)
-
-    def x_base(ref, axis, bit):
-        every, before = zero, zero
-        for i in range(NX):
-            t = ref[i]
-            every = every + t
-            before = before + jnp.where(i < x, t, 0.0)
-        return before + jnp.where(bit == 1, pltpu.roll(every, 1, axis), 0.0)
+    with jax.named_scope("wait_tp"):
+        receive(p_mate, p_order, tp, tp_r)
+    every, before = zero, zero
+    for i in range(NP):
+        t = tp[i]
+        every = every + t
+        before = before + jnp.where(i < p, t, 0.0)
+    v = every + pltpu.roll(before, 128 - NR, 1)
+    v = pltpu.roll(v, 0, 1, stride=NR, stride_axis=0)
+    v = jnp.sum(jnp.where(lane // NR == sub, v, 0.0), axis=0, keepdims=True)
+    vs[0] = v
+    vq[q] = v
+    send(q_mate, q_order, lambda o: vs.at[0], vq, vq_r, q, vq_s)
+
+    local_prefix(4, 7)
 
     with jax.named_scope("wait_x2"):
         receive(x_mate, x_order, x2, x2_r)
-    base = x_base(x2, 1, lane % 2)
+    every, before = zero, zero
+    for i in range(NX):
+        t = x2[i]
+        every = every + t
+        before = before + jnp.where(i < x, t, 0.0)
+    base = before + jnp.where(lane % 2 == 1, pltpu.roll(every, 1, 1), 0.0)
     for i in range(NZ):
         ps[i] = ps[i] + base
     ca[z] = ps[z]
     send(z_mate, z_order, lambda o: ps.at[o], ca, ca_r, z)
 
-    with jax.named_scope("wait_vz"):
-        receive(z_mate, z_order, vz, vz_r)
-    every, before = zero, zero
-    for i in range(NZ):
-        t = vz[i]
-        every = every + t
-        before = before + jnp.where(i < z, t, 0.0)
-    vt[...] = every
-    vx[x] = every
-    send(x_mate, x_order, lambda o: vt, vx, vx_r, x)
-
-    local_prefix(6, 7)
+    local_prefix(7, 8)
 
     with jax.named_scope("wait_cp"):
         receive(p_mate, p_order, cp, cp_r)
@@ -231,22 +221,32 @@
     for r in range(NR):
         cb[r] = cb[r] + jnp.where(bt_bit == 1, pltpu.roll(bt_ref[r], 2, 0), 0.0)
 
-    local_prefix(7, 8)
-
-    with jax.named_scope("wait_vx"):
-        receive(x_mate, x_order, vx, vx_r)
-    corner = before + x_base(vx, 0, sub % 2)
+    with jax.named_scope("wait_vq"):
+        receive(q_mate, q_order, vq, vq_r)
+    every, before = [0.0] * 4, [0.0] * 4
+    for i in range(NX * NZ):
+        t = vq[i]
+        every[i % 4] = every[i % 4] + t
+        before[i % 4] = before[i % 4] + jnp.where(i < q, t, 0.0)
+    every, before = [(t[0] + t[1]) + (t[2] + t[3]) for t in (every, before)]
+    every, before = [jnp.broadcast_to(t, (8, 128)) for t in (every, before)]
+    corner = before + jnp.where(lane // NR % 2 == 1, pltpu.roll(every, NR, 1), 0.0)
+    corner = jnp.where(lane // NR // 4 * 2 + lane // NR % 2 == sub // 4 * 2 + sub % 2, corner, 0.0)
     for r in range(NR):
-        bt_ref[r] = cb[r] + jnp.sum(jnp.where(lane == r, corner, 0.0), axis=1, keepdims=True)
+        bt_ref[r] = cb[r] + jnp.sum(jnp.where(lane % NR == r, corner, 0.0), axis=1, keepdims=True)
 
     with jax.named_scope("wait_ca"):
         receive(z_mate, z_order, ca, ca_r)
     carry_ref[...] = ca[...].reshape(8 * NR, 128)
-    tiles = 3 * len(z_order) + 2 * len(x_order) + (1 + NR) * len(p_order)
+    tiles = 2 * len(z_order) + len(x_order) + (1 + NR) * len(p_order)
     sent = l_ref.at[pl.ds(0, tiles * 8 // 2)]
     with jax.named_scope("wait_send"):
         pltpu.make_async_remote_copy(
             src_ref=sent, dst_ref=sent, send_sem=send_sem.at[0], recv_sem=z1_r.at[0],
+            device_id=z_mate(1)[1], device_id_type=MESH).wait_send()
+        sent = vq.at[pl.ds(0, len(q_order))]
+        pltpu.make_async_remote_copy(
+            src_ref=sent, dst_ref=sent, send_sem=vq_s.at[0], recv_sem=vq_r.at[0],
             device_id=z_mate(1)[1], device_id_type=MESH).wait_send()
 
 
@@ -262,16 +262,16 @@
 
     cf = [[lax.rsqrt(((c * NX * NZ + q) * B + bt * 128 + 1 + iota((8, 128), 1)).astype(F32)) for bt in range(2)] for c in range(NC)]
     first_row = (p * B + 1 + iota((8, 128), 0) * STEPS).astype(F32)
-    for r in range(NR):
+    def row_block(r, _):
         carry = av[r]
         offset = {}
         for n in range(NI):
             for c in range(NC):
+                own = e_ref[(n * NR + r) * NC + c]
                 for bt in range(2):
-                    own = e_ref[(n * NR + r) * NC + c][:, bt * 128:bt * 128 + 128]
-                    offset[n, c, bt] = own + bt_ref[r, pl.ds(n * 4 + bt * 2 + c, 1), :]
+                    offset[n, c, bt] = own[:, bt * 128:bt * 128 + 128] + bt_ref[r, pl.ds(n * 4 + bt * 2 + c, 1), :]
         for j in range(STEPS):
-            rf = lax.rsqrt(first_row + float(r * NP * B + j))
+            rf = lax.rsqrt(first_row + (r * NP * B + j).astype(F32))
             scale = [[rf * cf[c][bt] for bt in range(2)] for c in range(NC)]
             for n in range(NI):
                 k = n * NR + r
@@ -283,9 +283,12 @@
                         stage[pl.ds(k * 8 * PAD + j * 4 + c * 2 + bt, 8, stride=PAD), :] = (lv + (a + offset[n, c, bt])) * scale[c][bt]
         for n in range(NI):
             k = n * NR + r
-            for s in range(8):
+            for i in range(8):
                 pltpu.make_async_copy(
-                    stage.at[pl.ds((k * 8 + s) * PAD, SEG)], o_hbm.at[pl.ds((k * 8 + s) * SEG, SEG)], sem.at[0]).start()
+                    stage.at[pl.ds((k * 8 + i) * PAD, SEG)], o_hbm.at[pl.ds((k * 8 + i) * SEG, SEG)], sem.at[0]).start()
+        return 0
+
+    lax.fori_loop(0, NR, row_block, 0)
     pltpu.make_async_copy(stage.at[pl.ds(0, ROWS)], o_hbm, sem.at[0]).wait()
 
 
@@ -311,7 +314,8 @@
             pltpu.VMEM((2, 8 * PAD, 128), F32),
             tile(NR), tile(NR), tile(),
             tile(NZ), tile(NX), tile(NZ), tile(NZ), tile(),
-            tile(NP), tile(NP, NR), tile(), tile(NZ), tile(), tile(NX), tile(NR),
+            tile(NP), tile(NP, NR),
+            pltpu.VMEM((1, 1, 128), F32), pltpu.VMEM((NX * NZ, 1, 128), F32), tile(NR),
             dma((GROUPS,)),
         ] + [dma((1,))] * 8,
         compiler_params=pltpu.CompilerParams(collective_id=0, has_side_effects=True, vmem_limit_bytes=24 << 20),

time: 26.1 us -> 24.9 us (0.954)
  the two profiles are of different devices: /device:TPU:1 before, /device:TPU:8 now
where the time goes in v3:
time: 24.9 us; the launch traced here: 24.8 us
  Pallas kernels  24.8 us (100%)
    pallas_call x1, Pallas kernels, shards(): pl.pallas_call(scan_kernel, out_shape=(pltpu.VMEM((BLOCKS * B, B), F32),...  21.1 us
    pallas_call x1, Pallas kernels, shards(): pl.pallas_call(write_kernel, out_shape=pltpu.HBM((ROWS, 128), F32), in_sp...  3.72 us

profile of v3, /device:TPU:8, one launch (start us, length us, event | category | flops | bytes accessed | tf_op | source)
XLA Modules:
  0.0 24.8 jit_solution(3822177154381047673)
XLA Ops:
  0.0 21.1 %scan.1 = (f32[8192,256]{1,0:T(8,128)S(1)}, f32[32,8,256]{2,1,0:T(8,128)S(1)}, f32[64,128]{1,0:T(8,128)S(1)}, f32[8,8,128]{2,1,0:T(8,128)S(1)}) custom-call(bf16[16384,128]{1,0:T(8,128)(2,1)} %bitcast.6), custom_call_target="tpu_custom_call" | custom-call | tf_op jit(solution)/shard_map/scan/pallas_call | solution.py:302
  21.1 3.7 %write.1 = f32[16384,128]{1,0:T(8,128)} custom-call(f32[8192,256]{1,0:T(8,128)S(1)} %get-tuple-element.9.l_ref, f32[32,8,256]{2,1,0:T(8,128)S(1)} %get-tuple-element.10.e_ref, f32[64,128]{1,0:T(8,128)S(1)} %get-tuple-element.11.carry_ref, f32[8,8,128]{2,1,0:T(8,128)S(1)} %get-tuple-element.12.bt_ref), custom_call_target="tpu_custom_call" | custom-call | tf_op jit(solution)/shard_map/write/pallas_call | solution.py:324
